TPU v7x, 8 devices: a whole 2x2x1 slice. The times are simulated.
8 devices in a mesh: b: 1 (over z), rep: 2 (over y), col: 2 (over x), row: 2 (over core).
Axes of the slice: x: 2, y: 2, z: 1, core: 2. Of those that a mesh axis runs over, the one named last changes fastest.
Arguments:
- a_blocks: float32 [28, 28, 128, 128], P(('b', 'row'), 'col')
Outputs:
- output: float32 [28, 28, 128, 128], P(('b', 'row'), 'col')
All inputs are finite; a program needn't handle non-finite values.
Results may differ from a plain program's by a relative error of at most 0.001.
Values sent between devices are 32-bit elements.
A program may use at most 1 GiB of HBM per device.

v0:
```python
import jax
import jax.numpy as jnp
from jax import lax
from jax.sharding import PartitionSpec as P


def solution(mesh):
    row_size = mesh.shape["row"]
    col_size = mesh.shape["col"]
    rep_size = mesh.shape["rep"]
    grid_spec = P(("b", "row"), "col")

    def local_factor(a_loc):
        rows_blk, cols_blk, blk_size, _ = a_loc.shape
        num_steps = rows_blk * row_size
        share_len = blk_size // rep_size
        row_idx = lax.axis_index("row")
        col_idx = lax.axis_index("col")
        rep_idx = lax.axis_index("rep")
        work_mat = jnp.where(rep_idx == 0, a_loc, 0.0)
        out_cols = [jnp.zeros((rows_blk, blk_size, blk_size), jnp.float32)] * cols_blk
        for step_idx in range(num_steps):
            step_row = step_idx % row_size
            step_col = step_idx % col_size
            first_row = step_idx // row_size
            first_col = step_idx // col_size
            tail_rows = rows_blk - first_row
            col_sum = lax.psum(work_mat[first_row:, first_col], "rep")
            diag_mine = jnp.where(row_idx == step_row, col_sum[0], 0.0)
            diag_fac = jnp.tril(jnp.linalg.cholesky(lax.psum(diag_mine, "row")))
            solved = lax.linalg.triangular_solve(
                diag_fac, col_sum.reshape(tail_rows * blk_size, blk_size),
                left_side=False, lower=True, transpose_a=True,
            ).reshape(tail_rows, blk_size, blk_size)
            glob_row = ((first_row + jnp.arange(tail_rows)) * row_size + row_idx)[:, None, None]
            panel_blk = jnp.where(glob_row > step_idx, solved, jnp.where(glob_row == step_idx, diag_fac, 0.0))
            is_owner = col_idx == step_col
            padded = jnp.pad(panel_blk, ((first_row, 0), (0, 0), (0, 0)))
            out_cols[first_col] = jnp.where(is_owner, padded, out_cols[first_col])
            if step_idx < num_steps - 1:
                panel_row = lax.psum(jnp.where(is_owner, panel_blk, 0.0), "col")
                gathered = lax.all_gather(panel_row, "row", axis=1)
                col_full = jnp.pad(
                    gathered.reshape(tail_rows * row_size, blk_size, blk_size),
                    ((first_row * row_size, 0), (0, 0), (0, 0)),
                )
                col_grid = col_full.reshape(cols_blk, col_size, blk_size, blk_size)[first_col:]
                panel_col = lax.dynamic_index_in_dim(col_grid, col_idx, axis=1, keepdims=False)
                row_share = lax.dynamic_slice_in_dim(panel_row, rep_idx * share_len, share_len, axis=2)
                col_share = lax.dynamic_slice_in_dim(panel_col, rep_idx * share_len, share_len, axis=2)
                update = jnp.einsum(
                    "tak,uck->tuac", row_share, col_share,
                    precision=lax.Precision.HIGHEST, preferred_element_type=jnp.float32,
                )
                trail_new = work_mat[first_row:, first_col:] - update
                work_mat = lax.dynamic_update_slice(work_mat, trail_new, (first_row, first_col, 0, 0))
        return jnp.stack(out_cols, axis=1)

    return jax.shard_map(local_factor, mesh=mesh, in_specs=grid_spec, out_specs=grid_spec, check_vma=False)
```

profile of v0, /device:TPU:0, one launch (start us, length us, event | category | flops | bytes accessed | tf_op | source)
XLA Modules:
  0.0 2944.3 jit_solution(1216610518306682052)
XLA Ops:
  21.1 34.3 %all-reduce.110.cloned.1.call-done = f32[14,128,128]{2,1,0:T(8,128)} async-done(((f32[14,128,128]{2,1,0:T(8,128)}), f32[14,128,128]{2,1,0:T(8,128)}) %all-reduce.110.cloned.1.call-update) | async-done | bytes 917520 | tf_op jit(solution)/shard_map/psum | solution.py:28
  98.3 32.7 %all-reduce.114.cloned.1.call-done = f32[14,128,128]{2,1,0:T(8,128)} async-done(((f32[14,128,128]{2,1,0:T(8,128)}), f32[14,128,128]{2,1,0:T(8,128)}) %all-reduce.114.cloned.1.call-update) | async-done | bytes 917520 | tf_op jit(solution)/shard_map/psum | solution.py:41
  159.7 32.7 %all-reduce.116.cloned.1.call-done = f32[14,128,128]{2,1,0:T(8,128)} async-done(((f32[14,128,128]{2,1,0:T(8,128)}), f32[14,128,128]{2,1,0:T(8,128)}) %all-reduce.116.cloned.1.call-update) | async-done | bytes 917520 | tf_op jit(solution)/shard_map/psum | solution.py:28
  235.1 32.7 %all-reduce.120.cloned.1.call-done = f32[14,128,128]{2,1,0:T(8,128)} async-done(((f32[14,128,128]{2,1,0:T(8,128)}), f32[14,128,128]{2,1,0:T(8,128)}) %all-reduce.120.cloned.1.call-update) | async-done | bytes 917520 | tf_op jit(solution)/shard_map/psum | solution.py:41
  296.6 31.3 %all-reduce.122.cloned.1.call-done = f32[13,128,128]{2,1,0:T(8,128)} async-done(((f32[13,128,128]{2,1,0:T(8,128)}), f32[13,128,128]{2,1,0:T(8,128)}) %all-reduce.122.cloned.1.call-update) | async-done | bytes 851984 | tf_op jit(solution)/shard_map/psum | solution.py:28
  370.7 31.3 %all-reduce.126.cloned.1.call-done = f32[13,128,128]{2,1,0:T(8,128)} async-done(((f32[13,128,128]{2,1,0:T(8,128)}), f32[13,128,128]{2,1,0:T(8,128)}) %all-reduce.126.cloned.1.call-update) | async-done | bytes 851984 | tf_op jit(solution)/shard_map/psum | solution.py:41
  428.9 31.3 %all-reduce.128.cloned.1.call-done = f32[13,128,128]{2,1,0:T(8,128)} async-done(((f32[13,128,128]{2,1,0:T(8,128)}), f32[13,128,128]{2,1,0:T(8,128)}) %all-reduce.128.cloned.1.call-update) | async-done | bytes 851984 | tf_op jit(solution)/shard_map/psum | solution.py:28
  502.9 31.3 %all-reduce.132.cloned.1.call-done = f32[13,128,128]{2,1,0:T(8,128)} async-done(((f32[13,128,128]{2,1,0:T(8,128)}), f32[13,128,128]{2,1,0:T(8,128)}) %all-reduce.132.cloned.1.call-update) | async-done | bytes 851984 | tf_op jit(solution)/shard_map/psum | solution.py:41
  561.1 29.8 %all-reduce.134.cloned.1.call-done = f32[12,128,128]{2,1,0:T(8,128)} async-done(((f32[12,128,128]{2,1,0:T(8,128)}), f32[12,128,128]{2,1,0:T(8,128)}) %all-reduce.134.cloned.1.call-update) | async-done | bytes 786448 | tf_op jit(solution)/shard_map/psum | solution.py:28
  633.6 29.9 %all-reduce.138.cloned.1.call-done = f32[12,128,128]{2,1,0:T(8,128)} async-done(((f32[12,128,128]{2,1,0:T(8,128)}), f32[12,128,128]{2,1,0:T(8,128)}) %all-reduce.138.cloned.1.call-update) | async-done | bytes 786448 | tf_op jit(solution)/shard_map/psum | solution.py:41
  687.7 29.8 %all-reduce.140.cloned.1.call-done = f32[12,128,128]{2,1,0:T(8,128)} async-done(((f32[12,128,128]{2,1,0:T(8,128)}), f32[12,128,128]{2,1,0:T(8,128)}) %all-reduce.140.cloned.1.call-update) | async-done | bytes 786448 | tf_op jit(solution)/shard_map/psum | solution.py:28
  760.4 29.9 %all-reduce.144.cloned.1.call-done = f32[12,128,128]{2,1,0:T(8,128)} async-done(((f32[12,128,128]{2,1,0:T(8,128)}), f32[12,128,128]{2,1,0:T(8,128)}) %all-reduce.144.cloned.1.call-update) | async-done | bytes 786448 | tf_op jit(solution)/shard_map/psum | solution.py:41
  814.5 28.4 all-reduce.146.cloned.1.call-done
  885.5 28.4 all-reduce.150.cloned.1.call-done
  935.8 28.4 all-reduce.152.cloned.1.call-done
  1006.8 28.4 all-reduce.156.cloned.1.call-done
  1057.0 27.0 all-reduce.158.cloned.1.call-done
  1126.6 27.0 all-reduce.162.cloned.1.call-done
  1173.6 27.0 all-reduce.164.cloned.1.call-done
  1243.0 27.0 all-reduce.168.cloned.1.call-done
  1290.1 25.5 all-reduce.170.cloned.1.call-done
  1358.2 25.6 all-reduce.174.cloned.1.call-done
  1402.8 25.3 all-reduce.176.cloned.1.call-done
  1470.5 25.6 all-reduce.180.cloned.1.call-done
  1514.7 24.1 all-reduce.182.cloned.1.call-done
  1581.0 24.2 all-reduce.186.cloned.1.call-done
  1622.2 24.1 all-reduce.188.cloned.1.call-done
  1688.5 24.2 all-reduce.192.cloned.1.call-done
  1729.6 22.7 all-reduce.194.cloned.1.call-done
  1794.2 22.7 all-reduce.198.cloned.1.call-done
  1825.5 21.5 all-reduce.200.cloned.1.call-done
  1892.7 22.7 all-reduce.204.cloned.1.call-done
  (803 shorter events, 2040.5 us)
Async XLA Ops:
  56.9 74.1 %all-reduce.114.cloned.1.call-start = ((), (), s32[]{:S(2)}) async-start(), calls=%async_computation.2 | async-start | bytes 1835008 | tf_op jit(solution)/shard_map/psum | solution.py:41
  131.1 61.3 %all-reduce.116.cloned.1.call-start = ((), (), s32[]{:S(2)}) async-start(), calls=%async_computation.3 | async-start | bytes 1835008 | tf_op jit(solution)/shard_map/psum | solution.py:28
  193.9 74.0 %all-reduce.120.cloned.1.call-start = ((), (), s32[]{:S(2)}) async-start(), calls=%async_computation.5 | async-start | bytes 1835008 | tf_op jit(solution)/shard_map/psum | solution.py:41
  267.9 60.0 %all-reduce.122.cloned.1.call-start = ((), (), s32[]{:S(2)}) async-start(), calls=%async_computation.6 | async-start | bytes 1703936 | tf_op jit(solution)/shard_map/psum | solution.py:28
  329.4 72.6 %all-reduce.126.cloned.1.call-start = ((), (), s32[]{:S(2)}) async-start(), calls=%async_computation.8 | async-start | bytes 1703936 | tf_op jit(solution)/shard_map/psum | solution.py:41
  402.0 58.1 %all-reduce.128.cloned.1.call-start = ((), (), s32[]{:S(2)}) async-start(), calls=%async_computation.9 | async-start | bytes 1703936 | tf_op jit(solution)/shard_map/psum | solution.py:28
  461.7 72.6 %all-reduce.132.cloned.1.call-start = ((), (), s32[]{:S(2)}) async-start(), calls=%async_computation.11 | async-start | bytes 1703936 | tf_op jit(solution)/shard_map/psum | solution.py:41
  534.3 56.6 %all-reduce.134.cloned.1.call-start = ((), (), s32[]{:S(2)}) async-start(), calls=%async_computation.12 | async-start | bytes 1572864 | tf_op jit(solution)/shard_map/psum | solution.py:28
  592.4 71.0 %all-reduce.138.cloned.1.call-start = ((), (), s32[]{:S(2)}) async-start(), calls=%async_computation.14 | async-start | bytes 1572864 | tf_op jit(solution)/shard_map/psum | solution.py:41
  663.5 54.1 %all-reduce.140.cloned.1.call-start = ((), (), s32[]{:S(2)}) async-start(), calls=%async_computation.15 | async-start | bytes 1572864 | tf_op jit(solution)/shard_map/psum | solution.py:28
  719.0 71.2 %all-reduce.144.cloned.1.call-start = ((), (), s32[]{:S(2)}) async-start(), calls=%async_computation.17 | async-start | bytes 1572864 | tf_op jit(solution)/shard_map/psum | solution.py:41
  844.4 69.6 %all-reduce.150.cloned.1.call-start = ((), (), s32[]{:S(2)}) async-start(), calls=%async_computation.20 | async-start | bytes 1441792 | tf_op jit(solution)/shard_map/psum | solution.py:41
  965.7 69.6 %all-reduce.156.cloned.1.call-start = ((), (), s32[]{:S(2)}) async-start(), calls=%async_computation.23 | async-start | bytes 1441792 | tf_op jit(solution)/shard_map/psum | solution.py:41
  1085.5 68.1 %all-reduce.162.cloned.1.call-start = ((), (), s32[]{:S(2)}) async-start(), calls=%async_computation.26 | async-start | bytes 1310720 | tf_op jit(solution)/shard_map/psum | solution.py:41
  1202.0 68.0 %all-reduce.168.cloned.1.call-start = ((), (), s32[]{:S(2)}) async-start(), calls=%async_computation.29 | async-start | bytes 1310720 | tf_op jit(solution)/shard_map/psum | solution.py:41
  1317.2 66.6 %all-reduce.174.cloned.1.call-start = ((), (), s32[]{:S(2)}) async-start(), calls=%async_computation.32 | async-start | bytes 1179648 | tf_op jit(solution)/shard_map/psum | solution.py:41
  1429.6 66.4 %all-reduce.180.cloned.1.call-start = ((), (), s32[]{:S(2)}) async-start(), calls=%async_computation.35 | async-start | bytes 1179648 | tf_op jit(solution)/shard_map/psum | solution.py:41
  1540.3 64.9 %all-reduce.186.cloned.1.call-start = ((), (), s32[]{:S(2)}) async-start(), calls=%async_computation.38 | async-start | bytes 1048576 | tf_op jit(solution)/shard_map/psum | solution.py:41
  1647.8 64.9 %all-reduce.192.cloned.1.call-start = ((), (), s32[]{:S(2)}) async-start(), calls=%async_computation.41 | async-start | bytes 1048576 | tf_op jit(solution)/shard_map/psum | solution.py:41
  1753.8 63.1 %all-reduce.198.cloned.1.call-start = ((), (), s32[]{:S(2)}) async-start(), calls=%async_computation.44 | async-start | bytes 917504 | tf_op jit(solution)/shard_map/psum | solution.py:41
  1848.5 66.8 %all-reduce.204.cloned.1.call-start = ((), (), s32[]{:S(2)}) async-start(), calls=%async_computation.47 | async-start | bytes 917504 | tf_op jit(solution)/shard_map/psum | solution.py:41
  1946.2 61.7 %all-reduce.210.cloned.1.call-start = ((), (), s32[]{:S(2)}) async-start(), calls=%async_computation.50 | async-start | bytes 786432 | tf_op jit(solution)/shard_map/psum | solution.py:41
  2036.8 61.5 %all-reduce.216.cloned.1.call-start = ((), (), s32[]{:S(2)}) async-start(), calls=%async_computation.53 | async-start | bytes 786432 | tf_op jit(solution)/shard_map/psum | solution.py:41
  2126.3 60.1 %all-reduce.222.cloned.1.call-start = ((), (), s32[]{:S(2)}) async-start(), calls=%async_computation.56 | async-start | bytes 655360 | tf_op jit(solution)/shard_map/psum | solution.py:41
  2212.8 60.1 %all-reduce.228.cloned.1.call-start = ((), (), s32[]{:S(2)}) async-start(), calls=%async_computation.59 | async-start | bytes 655360 | tf_op jit(solution)/shard_map/psum | solution.py:41
  2297.5 58.7 %all-reduce.234.cloned.1.call-start = ((), (), s32[]{:S(2)}) async-start(), calls=%async_computation.62 | async-start | bytes 524288 | tf_op jit(solution)/shard_map/psum | solution.py:41
  2381.3 58.9 %all-reduce.240.cloned.1.call-start = ((), (), s32[]{:S(2)}) async-start(), calls=%async_computation.65 | async-start | bytes 524288 | tf_op jit(solution)/shard_map/psum | solution.py:41
  2465.0 68.2 %all-reduce.246.cloned.1.call-start = ((), (), s32[]{:S(2)}) async-start(), calls=%async_computation.68 | async-start | bytes 393216 | tf_op jit(solution)/shard_map/psum | solution.py:41
  2556.9 69.3 %all-reduce.252.cloned.1.call-start = ((), (), s32[]{:S(2)}) async-start(), calls=%async_computation.71 | async-start | bytes 393216 | tf_op jit(solution)/shard_map/psum | solution.py:41
  2649.1 56.7 %all-reduce.258.cloned.1.call-start = ((), (), s32[]{:S(2)}) async-start(), calls=%async_computation.74 | async-start | bytes 262144 | tf_op jit(solution)/shard_map/psum | solution.py:41
  2728.1 58.4 %all-reduce.264.cloned.1.call-start = ((), (), s32[]{:S(2)}) async-start(), calls=%async_computation.77 | async-start | bytes 262144 | tf_op jit(solution)/shard_map/psum | solution.py:41
  2808.3 56.6 %all-reduce.270.cloned.1.call-start = ((), (), s32[]{:S(2)}) async-start(), calls=%async_computation.80 | async-start | bytes 131072 | tf_op jit(solution)/shard_map/psum | solution.py:41
  (116 other events, 5813.6 us)
Sparse Core Ops, SparseCore 0:
  21.2 34.2 all-reduce.109
  98.4 32.5 all-reduce.113
  159.8 32.5 all-reduce.115
  235.2 32.5 all-reduce.119
  296.7 31.1 all-reduce.121
  370.8 31.1 all-reduce.125
  429.0 31.1 all-reduce.127
  503.0 31.1 all-reduce.131
  561.2 29.7 all-reduce.133
  633.6 29.7 all-reduce.137
  687.8 29.7 all-reduce.139
  760.4 29.7 all-reduce.143
  814.5 28.2 all-reduce.145
  885.6 28.3 all-reduce.149
  935.8 28.2 all-reduce.151
  1006.9 28.3 all-reduce.155
  1057.1 26.8 all-reduce.157
  1126.6 26.8 all-reduce.161
  1173.6 26.8 all-reduce.163
  1243.1 26.8 all-reduce.167
  1290.2 25.4 all-reduce.169
  1358.3 25.4 all-reduce.173
  1402.6 25.4 all-reduce.175
  1470.5 25.4 all-reduce.179
  1514.7 23.9 all-reduce.181
  1581.1 24.0 all-reduce.185
  1622.2 23.9 all-reduce.187
  1688.6 24.0 all-reduce.191
  1729.7 22.5 all-reduce.193
  1794.3 22.5 all-reduce.197
  1825.6 21.4 all-reduce.199
  1892.7 22.5 all-reduce.203
  (65 shorter events, 841.1 us)
where the time goes:
time: 2960 us; the launch traced here: 2940 us
  waiting for transfers between devices  1750 us (59%)
  other arithmetic  785 us (27%)
  matrix products  223 us (8%)
  local copies, waits for them, and re-layouts  131 us (4%)
    psum x28, waiting for transfers between devices, local_factor(): col_sum = lax.psum(work_mat[first_row:, first_col], 'rep')  645 us
    psum x27, waiting for transfers between devices, local_factor(): panel_row = lax.psum(jnp.where(is_owner, panel_blk, 0.0), 'col')  643 us
    another operation x84, other arithmetic, local_factor(): diag_fac = jnp.tril(jnp.linalg.cholesky(lax.psum(diag_mine, 'row')))  353 us
    psum x28, waiting for transfers between devices, local_factor(): diag_fac = jnp.tril(jnp.linalg.cholesky(lax.psum(diag_mine, 'row')))  345 us
    another operation x56, other arithmetic, local_factor(): lax.linalg.triangular_solve(diag_fac, col_sum.reshape(tail_rows * blk_siz...  299 us
    dot_general x27, matrix products, local_factor(): jnp.einsum('tak,uck->tuac', row_share, col_share, precision=lax.Precision...  174 us
    all_gather x14, waiting for transfers between devices, local_factor(): gathered = lax.all_gather(panel_row, 'row', axis=1)  112 us
  transfers between devices with their start and end apart: 97, of which 97 were waited for; matrix products, arithmetic and copies ran while one was open for 1% of the time, Pallas kernels for 0%

commit v1 on v0

v1 whole, which is shorter than its diff:
```python
import functools

import jax
import jax.numpy as jnp
from jax import lax
from jax.experimental import pallas as pl
from jax.experimental.pallas import tpu as pltpu
from jax.sharding import PartitionSpec as P

NB = 128
SUB = 8
F32 = jnp.float32
BF16 = jnp.bfloat16


def split3(x):
    hi = x.astype(BF16)
    rest = x - hi.astype(F32)
    mid = rest.astype(BF16)
    low = (rest - mid.astype(F32)).astype(BF16)
    return hi, mid, low


def dot_nt(a, b):
    return lax.dot_general(a, b, (((1,), (1,)), ((), ())), preferred_element_type=F32)


def dot_nn(a, b):
    return lax.dot_general(a, b, (((1,), (0,)), ((), ())), preferred_element_type=F32)


def six(dot, a, b):
    ah, am, al = a
    bh, bm, bl = b
    small = dot(al, bh) + dot(ah, bl) + dot(am, bm)
    return (small + (dot(am, bh) + dot(ah, bm))) + dot(ah, bh)


def factor_rows(cols, rows):
    sub = lax.broadcasted_iota(jnp.int32, (SUB, NB), 0)
    for k in range(SUB):
        inv_root = lax.rsqrt(jnp.broadcast_to(cols[k][k:k + 1, :], (SUB, NB)))
        scaled = cols[k] * inv_root
        mult = jnp.where(sub > k, scaled, 0.0)
        for c in range(k + 1, SUB):
            cols[c] = cols[c] - scaled * jnp.broadcast_to(scaled[c:c + 1, :], (SUB, NB))
        new_rows = []
        for row in rows:
            pivot_row = jnp.broadcast_to(row[k:k + 1, :], (SUB, NB)) * inv_root
            new_rows.append(jnp.where(sub == k, pivot_row, row - mult * pivot_row))
        rows = new_rows
    return rows


def factor_block(slabs):
    steps = NB // SUB
    sub = lax.broadcasted_iota(jnp.int32, (SUB, NB), 0)
    lane = lax.broadcasted_iota(jnp.int32, (SUB, NB), 1)
    rows = [[slabs[t], jnp.where(lane == sub + SUB * t, 1.0, 0.0).astype(F32)] for t in range(steps)]
    cols = [jnp.broadcast_to(rows[0][0][:, c:c + 1], (SUB, NB)) for c in range(SUB)]
    for t in range(steps):
        rows[t] = factor_rows(cols, rows[t])
        for s in range(t + 1, steps):
            index = sub + SUB * s
            fac, inv = rows[s]
            if s == t + 1:
                cols = [jnp.broadcast_to(fac[:, SUB * s + c:SUB * s + c + 1], (SUB, NB)) for c in range(SUB)]
            for k in range(SUB):
                fac_row = jnp.broadcast_to(rows[t][0][k:k + 1, :], (SUB, NB))
                inv_row = jnp.broadcast_to(rows[t][1][k:k + 1, :], (SUB, NB))
                col = jnp.take_along_axis(fac_row, index, axis=1)
                fac = fac - col * fac_row
                inv = inv - col * inv_row
                if s == t + 1:
                    for c in range(SUB):
                        cols[c] = cols[c] - col * jnp.broadcast_to(col[c:c + 1, :], (SUB, NB))
            rows[s] = [fac, inv]
    upper = [jnp.where(lane >= sub + SUB * t, rows[t][0], 0.0) for t in range(steps)]
    inverse = [jnp.where(lane <= sub + SUB * t, rows[t][1], 0.0) for t in range(steps)]
    return upper, inverse


def kernel(n, src, out, tiles, hi, mid, low, invs, upper, blk_inv, zero, in_sem, out_sem, zero_sem):
    W = 2 * NB
    my_row = lax.axis_index("row")
    my_col = lax.axis_index("col")

    def col_start(p):
        return p * n - (p * (p - 1)) // 2

    def tile_row(big, p):
        return pl.multiple_of((col_start(p) + big - p) * W, W)

    def load_tile(p, big):
        row = tile_row(big, p)
        for r in range(2):
            for c in range(2):
                pltpu.make_async_copy(
                    src.at[r, c, big, p],
                    tiles.at[pl.ds(row + r * NB, NB), pl.ds(c * NB, NB)],
                    in_sem.at[p],
                ).start()

    zero[...] = jnp.zeros_like(zero)

    @pl.loop(0, n)
    def _(p):
        @pl.loop(p, n)
        def _(big):
            load_tile(p, big)

    @pl.loop(0, n)
    def _(p):
        @pl.loop(0, p)
        def _(big):
            pltpu.make_async_copy(zero, out.at[big, p], zero_sem).start()

    @pl.loop(0, n)
    def _(p):
        @pl.loop(p, n)
        def _(big):
            ref = tiles.at[pl.ds(tile_row(big, p), W), :]
            pltpu.make_async_copy(ref, ref, in_sem.at[p]).wait()

    def factor(row, off, which):
        up, inv = factor_block([tiles[pl.ds(row + off + SUB * t, SUB), pl.ds(off, NB)] for t in range(NB // SUB)])
        for t in range(NB // SUB):
            upper[SUB * t:SUB * (t + 1), :] = up[t]
            blk_inv[which, SUB * t:SUB * (t + 1), :] = inv[t]
        tiles[pl.ds(row + off, NB), pl.ds(off, NB)] = upper[...].T

    @pl.loop(0, n)
    def _(s):
        row = tile_row(s, s)
        factor(row, 0, 0)
        inv1 = split3(blk_inv[0])
        l21 = six(dot_nt, split3(tiles[pl.ds(row + NB, NB), 0:NB]), inv1)
        tiles[pl.ds(row + NB, NB), 0:NB] = l21
        l21_parts = split3(l21)
        tiles[pl.ds(row + NB, NB), NB:W] = tiles[pl.ds(row + NB, NB), NB:W] - six(dot_nt, l21_parts, l21_parts)
        factor(row, NB, 1)
        tiles[pl.ds(row, NB), NB:W] = jnp.zeros((NB, NB), F32)
        inv2 = split3(blk_inv[1])
        cross = six(dot_nn, split3(six(dot_nn, inv2, l21_parts)), inv1)
        for part in range(3):
            invs[part, 0:NB, 0:NB] = inv1[part]
            invs[part, NB:W, NB:W] = inv2[part]
            invs[part, 0:NB, NB:W] = jnp.zeros((NB, NB), BF16)
        for part, val in enumerate(split3(-cross)):
            invs[part, NB:W, 0:NB] = val

        @pl.loop(s + 1, n)
        def _(big):
            trow = tile_row(big, s)
            a = split3(tiles[pl.ds(trow, W), :])
            sol = six(dot_nt, a, (invs[0], invs[1], invs[2]))
            tiles[pl.ds(trow, W), :] = sol
            h, m, l = split3(sol)
            prow = pl.multiple_of(big * W, W)
            hi[pl.ds(prow, W), :] = h
            mid[pl.ds(prow, W), :] = m
            low[pl.ds(prow, W), :] = l

        @pl.loop(s, n)
        def _(big):
            pltpu.make_async_copy(
                tiles.at[pl.ds(tile_row(big, s) + pl.multiple_of(my_row * NB, NB), NB), pl.ds(pl.multiple_of(my_col * NB, NB), NB)],
                out.at[big, s],
                out_sem,
            ).start()

        @pl.loop(s + 1, n)
        def _(p):
            prow = pl.multiple_of(p * W, W)
            @pl.loop(p, n)
            def _(big):
                brow = pl.multiple_of(big * W, W)
                a = tuple(ref[pl.ds(brow, W), :] for ref in (hi, mid, low))
                b = tuple(ref[pl.ds(prow, W), :] for ref in (hi, mid, low))
                trow = tile_row(big, p)
                tiles[pl.ds(trow, W), :] = tiles[pl.ds(trow, W), :] - six(dot_nt, a, b)

    @pl.loop(0, n)
    def _(p):
        @pl.loop(p, n)
        def _(big):
            pltpu.make_async_copy(
                tiles.at[pl.ds(tile_row(big, p) + pl.multiple_of(my_row * NB, NB), NB), pl.ds(pl.multiple_of(my_col * NB, NB), NB)],
                out.at[big, p],
                out_sem,
            ).wait()

    @pl.loop(0, n)
    def _(p):
        @pl.loop(0, p)
        def _(big):
            pltpu.make_async_copy(zero, out.at[big, p], zero_sem).wait()


def solution(mesh):
    grid_spec = P(("b", "row"), "col")

    def local_factor(a_loc):
        n = a_loc.shape[0]
        W = 2 * NB
        gathered = lax.all_gather(lax.all_gather(a_loc, "col"), "row")
        return pl.pallas_call(
            functools.partial(kernel, n),
            out_shape=jax.ShapeDtypeStruct(a_loc.shape, F32),
            in_specs=[pl.BlockSpec(memory_space=pl.ANY)],
            out_specs=pl.BlockSpec(memory_space=pl.ANY),
            scratch_shapes=[
                pltpu.VMEM((n * (n + 1) // 2 * W, W), F32),
                pltpu.VMEM((n * W, W), BF16),
                pltpu.VMEM((n * W, W), BF16),
                pltpu.VMEM((n * W, W), BF16),
                pltpu.VMEM((3, W, W), BF16),
                pltpu.VMEM((NB, NB), F32),
                pltpu.VMEM((2, NB, NB), F32),
                pltpu.VMEM((NB, NB), F32),
                pltpu.SemaphoreType.DMA((n,)),
                pltpu.SemaphoreType.DMA,
                pltpu.SemaphoreType.DMA,
            ],
            compiler_params=pltpu.CompilerParams(vmem_limit_bytes=60 << 20),
        )(gathered)

    return jax.shard_map(local_factor, mesh=mesh, in_specs=grid_spec, out_specs=grid_spec, check_vma=False)
```

time: 2960 us -> 721 us (0.24)
  waiting for transfers between devices: 1750 us -> 378 us
  other arithmetic: 785 us -> 0 us
  Pallas kernels: 0 us -> 329 us
  matrix products: 223 us -> 0 us
  local copies, waits for them, and re-layouts: 131 us -> 0 us
    psum x83 -> x0, waiting for transfers between devices: 1630 us -> none  [the longest x28 645 us: local_factor(): col_sum = lax.psum(work_mat[first_row:, first_col], 'rep')]
    another operation x141 -> x0, other arithmetic: 652 us -> none  [the longest x84 353 us: local_factor(): diag_fac = jnp.tril(jnp.linalg.cholesky(lax.psum(diag_mine, 'row')))]
    pallas_call x0 -> x1, Pallas kernels: none -> 329 us  [local_factor(): pl.pallas_call(functools.partial(kernel, n), out_shape=jax.ShapeDtypeStru...]
    all_gather x14 -> x2, waiting for transfers between devices: 112 us -> 378 us  [local_factor(): gathered = lax.all_gather(lax.all_gather(a_loc, 'col'), 'row')]
    dot_general x27 -> x0, matrix products: 174 us -> none  [local_factor(): jnp.einsum('tak,uck->tuac', row_share, col_share, precision=lax.Precision...]
    select_n x56 -> x0, other arithmetic: 86.1 us -> none  [the longest x28 40.2 us: local_factor(): diag_mine = jnp.where(row_idx == step_row, col_sum[0], 0.0)]
    unnamed x102 -> x0, local copies, waits for them, and re-layouts: 54 us -> none
    another operation x28 -> x0, matrix products: 49.5 us -> none  [local_factor(): lax.linalg.triangular_solve(diag_fac, col_sum.reshape(tail_rows * blk_siz...]
  transfers between devices with their start and end apart: 97 -> 2, of which waited for: 97 -> 2; matrix products, arithmetic and copies ran while one was open for 1% -> 0% of each run, Pallas kernels for 0% -> 0%
where the time goes in v1:
time: 721 us
  waiting for transfers between devices  378 us (52%)
  Pallas kernels  329 us (46%)
  between operations  13.4 us (2%)
    all_gather x2, waiting for transfers between devices, local_factor(): gathered = lax.all_gather(lax.all_gather(a_loc, 'col'), 'row')  378 us
    pallas_call x1, Pallas kernels, local_factor(): pl.pallas_call(functools.partial(kernel, n), out_shape=jax.ShapeDtypeStru...  329 us
  transfers between devices with their start and end apart: 2, of which 2 were waited for; matrix products, arithmetic and copies ran while one was open for 0% of the time, Pallas kernels for 0%

profile of v1, /device:TPU:0, one launch (start us, length us, event | category | flops | bytes accessed | tf_op | source)
XLA Modules:
  0.0 720.8 jit_solution(6354517780946552994)
XLA Ops:
  6.5 0.0 all-gather.5.cloned.1.call-start
  6.5 0.7 all-gather.5.cloned.1.call-update
  7.3 0.0 all-gather.7.cloned.1.call-start
  7.3 303.5 %all-gather.5.cloned.1.call-done = f32[28,14,128,128]{3,2,1,0:T(8,128)} async-done(((f32[14,14,128,128]{3,2,1,0:T(8,128)}), f32[28,14,128,128]{3,2,1,0:T(8,128)}) %all-gather.5.cloned.1.call-update) | async-done | bytes 25690128 | tf_op jit(solution)/shard_map/all_gather | solution.py:206
  310.8 0.0 all-gather.7.cloned.1.call-update
  310.9 74.0 %all-gather.7.cloned.1.call-done = f32[4,14,14,128,128]{4,3,2,1,0:T(8,128)} async-done(((f32[2,14,14,128,128]{4,3,2,1,0:T(8,128)}), f32[4,14,14,128,128]{4,3,2,1,0:T(8,128)}) %all-gather.7.cloned.1.call-update) | async-done | bytes 51380240 | tf_op jit(solution)/shard_map/all_gather | solution.py:206
  384.9 329.1 %shard_map.17 = f32[14,14,128,128]{3,2,1,0:T(8,128)} custom-call(f32[2,2,14,14,128,128]{5,4,3,2,1,0:T(8,128)} %bitcast.2), custom_call_target="tpu_custom_call" | custom-call | tf_op jit(solution)/shard_map/pallas_call | solution.py:207
Async XLA Ops:
  6.5 304.3 %all-gather.5.cloned.1.call-start = ((), (), s32[]{:S(2)}) async-start(), calls=%async_computation | async-start | bytes 38535168 | tf_op jit(solution)/shard_map/all_gather | solution.py:206
  7.3 377.6 %all-gather.7.cloned.1.call-start = ((), (), s32[]{:S(2)}) async-start(), calls=%async_computation.1 | async-start | bytes 77070336 | tf_op jit(solution)/shard_map/all_gather | solution.py:206
Sparse Core Ops, SparseCore 0:
  8.9 301.9 all-gather.4
  312.4 72.4 all-gather.6

commit v2 on v1

v2 whole, which is shorter than its diff:
```python
import functools

import jax
import jax.numpy as jnp
from jax import lax
from jax.experimental import pallas as pl
from jax.experimental.pallas import tpu as pltpu
from jax.sharding import PartitionSpec as P

NB = 128
SUB = 8
F32 = jnp.float32
BF16 = jnp.bfloat16


def split3(x):
    hi = x.astype(BF16)
    rest = x - hi.astype(F32)
    mid = rest.astype(BF16)
    low = (rest - mid.astype(F32)).astype(BF16)
    return hi, mid, low


def dot_nt(a, b):
    return lax.dot_general(a, b, (((1,), (1,)), ((), ())), preferred_element_type=F32)


def dot_nn(a, b):
    return lax.dot_general(a, b, (((1,), (0,)), ((), ())), preferred_element_type=F32)


def six(dot, a, b):
    ah, am, al = a
    bh, bm, bl = b
    small = dot(al, bh) + dot(ah, bl) + dot(am, bm)
    return (small + (dot(am, bh) + dot(ah, bm))) + dot(ah, bh)


def spread_row(x, k):
    return jnp.broadcast_to(x[k:k + 1, :], (SUB, NB))


def spread_cols(x, first):
    return [jnp.broadcast_to(x[:, first + c:first + c + 1], (SUB, NB)) for c in range(SUB)]


def factor_block(load, store):
    steps = NB // SUB
    sub = lax.broadcasted_iota(jnp.int32, (SUB, NB), 0)
    lane = lax.broadcasted_iota(jnp.int32, (SUB, NB), 1)
    rows = [[load(t), jnp.where(lane == sub + SUB * t, 1.0, 0.0).astype(F32)] for t in range(steps)]
    main = spread_cols(rows[0][0], 0)
    ext = spread_cols(rows[1][0], 0)
    for t in range(steps):
        fac, inv = rows[t]
        fac_rows, inv_rows, below = [], [], []
        for k in range(SUB):
            inv_root = lax.rsqrt(spread_row(main[k], k))
            scaled = main[k] * inv_root
            scaled_ext = ext[k] * inv_root if t + 1 < steps else None
            below.append(scaled_ext)
            for c in range(k + 1, SUB):
                factor_c = spread_row(scaled, c)
                main[c] = main[c] - scaled * factor_c
                if t + 1 < steps:
                    ext[c] = ext[c] - scaled_ext * factor_c
            mult = jnp.where(sub > k, scaled, 0.0)
            fac_row = spread_row(fac, k) * inv_root
            inv_row = spread_row(inv, k) * inv_root
            fac = jnp.where(sub == k, fac_row, fac - mult * fac_row)
            inv = jnp.where(sub == k, inv_row, inv - mult * inv_row)
            fac_rows.append(fac_row)
            inv_rows.append(inv_row)
        store(t, jnp.where(lane >= sub + SUB * t, fac, 0.0), jnp.where(lane <= sub + SUB * t, inv, 0.0))
        if t + 1 == steps:
            break
        s = t + 1
        next_main = spread_cols(rows[s][0], SUB * s)
        for k in range(SUB):
            rows[s][0] = rows[s][0] - below[k] * fac_rows[k]
            rows[s][1] = rows[s][1] - below[k] * inv_rows[k]
            for c in range(SUB):
                next_main[c] = next_main[c] - below[k] * spread_row(below[k], c)
        if s + 1 < steps:
            turned = fac.T
            next_ext = spread_cols(rows[s + 1][0], SUB * s)
            for q in range(t + 2, steps):
                for k in range(SUB):
                    col = jnp.broadcast_to(turned[SUB * q:SUB * (q + 1), k:k + 1], (SUB, NB))
                    rows[q][0] = rows[q][0] - col * fac_rows[k]
                    rows[q][1] = rows[q][1] - col * inv_rows[k]
                    if q == t + 2:
                        for c in range(SUB):
                            next_ext[c] = next_ext[c] - col * spread_row(below[k], c)
            ext = next_ext
        main = next_main


def kernel(n, src, out, tiles, hi, mid, low, invs, upper, blk, blk_inv, zero,
           loc_sem, sib_sem, nbr_sem, panel_sem, diag_sem, diag_send_sem, block_send_sem, panel_send_sem,
           out_sem, zero_sem):
    W = 2 * NB
    my_row = lax.axis_index("row")
    my_col = lax.axis_index("col")
    sibling = {"row": 1 - my_row}
    aligned = my_row == my_col
    num_own = n // 2

    barrier = pltpu.get_barrier_semaphore()
    pl.semaphore_signal(barrier, inc=1, device_id=sibling, device_id_type=pl.DeviceIdType.MESH)
    for core in range(2):
        pl.semaphore_signal(barrier, inc=1, device_id={"col": 1 - my_col, "row": core},
                            device_id_type=pl.DeviceIdType.MESH)
    pl.semaphore_wait(barrier, 3)

    def tile_row(big, p):
        return pl.multiple_of((p * n - (p * (p - 1)) // 2 + big - p) * W, W)

    def quadrant(big, p, r, c):
        return tiles.at[pl.ds(pl.multiple_of(tile_row(big, p) + r * NB, NB), NB), pl.ds(pl.multiple_of(c * NB, NB), NB)]

    def tile_ref(big, p):
        return tiles.at[pl.ds(tile_row(big, p), W), :]

    def first_own(p):
        return p + lax.rem(p + my_row, 2)

    def first_other(p):
        return p + lax.rem(p + 1 + my_row, 2)

    def own_tiles(p):
        first = first_own(p)
        return first, lax.div(n + 1 - first, 2)

    def other_tiles(p):
        first = first_other(p)
        return first, lax.div(n + 1 - first, 2)

    def own_loop(p, fn):
        first, count = own_tiles(p)

        @pl.loop(0, count)
        def _(q):
            fn(first + 2 * q)

    def other_loop(p, fn):
        first, count = other_tiles(p)

        @pl.loop(0, count)
        def _(q):
            fn(first + 2 * q)

    def local_copy(block, dst, big, p):
        return pltpu.make_async_copy(block, dst, loc_sem.at[p, lax.div(big, 2)])

    def remote(block, dst, recv, send, device):
        return pltpu.make_async_remote_copy(
            src_ref=block, dst_ref=dst, send_sem=send, recv_sem=recv,
            device_id=device, device_id_type=pl.DeviceIdType.MESH)

    zero[...] = jnp.zeros_like(zero)

    @pl.loop(0, n)
    def _(p):
        def own(big):
            local_copy(src.at[big, p], quadrant(big, p, my_row, my_col), big, p).start()

            @pl.when(jnp.logical_not(aligned))
            def _():
                local_copy(src.at[p, big], quadrant(big, p, my_col, my_row), big, p).start()

        def other(big):
            remote(src.at[big, p], quadrant(big, p, my_row, my_col), sib_sem.at[p, lax.div(big, 2)], block_send_sem, sibling).start()

            @pl.when(jnp.logical_not(aligned))
            def _():
                remote(src.at[p, big], quadrant(big, p, my_col, my_row), sib_sem.at[p, lax.div(big, 2)], block_send_sem, sibling).start()

        own_loop(p, own)
        other_loop(p, other)

        @pl.when(aligned)
        def _():
            @pl.loop(p, n)
            def _(big):
                remote(src.at[big, p], quadrant(big, p, my_row, my_col), nbr_sem.at[p, lax.div(big, 2)], block_send_sem,
                       {"col": 1 - my_col, "row": lax.rem(big, 2)}).start()

    @pl.loop(0, n)
    def _(p):
        @pl.loop(0, p)
        def _(big):
            pltpu.make_async_copy(zero, out.at[big, p], zero_sem).start()

    def wait_blocks(count, sem):
        ref = tiles.at[pl.ds(0, count * NB // 2), :]
        pltpu.make_async_copy(ref, ref, sem).wait()

    def arrive(p):
        def own(big):
            half = lax.div(big, 2)
            wait_blocks(1, nbr_sem.at[p, half])

            @pl.when(aligned)
            def _():
                wait_blocks(1, loc_sem.at[p, half])
                wait_blocks(2, sib_sem.at[p, half])

            @pl.when(jnp.logical_not(aligned))
            def _():
                wait_blocks(2, loc_sem.at[p, half])
                wait_blocks(1, sib_sem.at[p, half])

        own_loop(p, own)

        def turn(big):
            for c in range(2):
                @pl.when(my_col == c)
                def _():
                    rows = pl.ds(tile_row(big, p) + c * NB, NB)
                    lanes = slice((1 - c) * NB, (2 - c) * NB)
                    tiles[rows, lanes] = tiles[rows, lanes].T

        own_loop(p, turn)

    def factor(which):
        def store(t, up, inv):
            upper[SUB * t:SUB * (t + 1), :] = up
            blk_inv[which, SUB * t:SUB * (t + 1), :] = inv

        factor_block(lambda t: blk[SUB * t:SUB * (t + 1), :], store)

    def parts(ref_row):
        row = pl.multiple_of(ref_row * W, W)
        return tuple(ref[pl.ds(row, W), :] for ref in (hi, mid, low))

    def keep_parts(big, value):
        row = pl.multiple_of(big * W, W)
        for ref, val in zip((hi, mid, low), split3(value)):
            ref[pl.ds(row, W), :] = val

    def diag_copy(s):
        return remote(tile_ref(s, s), tile_ref(s, s), diag_sem.at[s], diag_send_sem.at[s], sibling)

    def panel_copy(big, s):
        return remote(tile_ref(big, s), tile_ref(big, s), panel_sem.at[s, lax.div(big, 2)], panel_send_sem.at[lax.div(big, 2)], sibling)

    def update(big, p, rhs):
        trow = tile_row(big, p)
        tiles[pl.ds(trow, W), :] = tiles[pl.ds(trow, W), :] - six(dot_nt, parts(big), rhs)

    def own(s):
        return lax.rem(s, 2) == my_row

    arrive(0)

    @pl.when(own(0))
    def _():
        diag_copy(0).start()

    @pl.loop(0, n)
    def _(s):
        @pl.when(own(s))
        def _():
            diag_copy(s).wait_send()

        @pl.when(jnp.logical_not(own(s)))
        def _():
            diag_copy(s).wait_recv()

        row = tile_row(s, s)
        top, bottom = pl.ds(row, NB), pl.ds(row + NB, NB)

        @pl.loop(0, 2)
        def _(half):
            @pl.when(half == 0)
            def _():
                blk[...] = tiles[top, 0:NB]

            @pl.when(half == 1)
            def _():
                below = six(dot_nt, split3(tiles[bottom, 0:NB]), split3(blk_inv[0]))
                tiles[bottom, 0:NB] = below
                pieces = split3(below)
                blk[...] = tiles[bottom, NB:W] - six(dot_nt, pieces, pieces)

            factor(half)

            @pl.when(half == 0)
            def _():
                tiles[top, 0:NB] = upper[...].T

            @pl.when(half == 1)
            def _():
                tiles[bottom, NB:W] = upper[...].T

        tiles[top, NB:W] = jnp.zeros((NB, NB), F32)
        l21_parts = split3(tiles[bottom, 0:NB])
        inv1, inv2 = split3(blk_inv[0]), split3(blk_inv[1])
        cross = six(dot_nn, split3(six(dot_nn, inv2, l21_parts)), inv1)
        for part in range(3):
            invs[part, 0:NB, 0:NB] = inv1[part]
            invs[part, NB:W, NB:W] = inv2[part]
            invs[part, 0:NB, NB:W] = jnp.zeros((NB, NB), BF16)
        for part, val in enumerate(split3(-cross)):
            invs[part, NB:W, 0:NB] = val

        def solve(big):
            trow = tile_row(big, s)
            sol = six(dot_nt, split3(tiles[pl.ds(trow, W), :]), (invs[0], invs[1], invs[2]))
            tiles[pl.ds(trow, W), :] = sol
            panel_copy(big, s).start()
            keep_parts(big, sol)

        own_loop(s + 1, solve)

        @pl.when(jnp.logical_and(s == 0, s + 1 < n))
        def _():
            arrive(1)

        @pl.when(jnp.logical_and(own(s + 1), s + 1 < n))
        def _():
            update(s + 1, s + 1, parts(s + 1))
            diag_copy(s + 1).start()

        other_loop(s + 1, lambda big: panel_copy(big, s).wait_recv())
        other_loop(s + 1, lambda big: keep_parts(big, tiles[pl.ds(tile_row(big, s), W), :]))

        @pl.loop(s, n)
        def _(big):
            pltpu.make_async_copy(quadrant(big, s, my_row, my_col), out.at[big, s], out_sem).start()

        @pl.loop(s + 1, n)
        def _(p):
            @pl.when(jnp.logical_and(s == 0, p > 1))
            def _():
                arrive(p)

            first, count = own_tiles(p)
            done = jnp.logical_and(p == s + 1, own(p)).astype(jnp.int32)
            first = first + 2 * done
            count = count - done

            @pl.loop(0, lax.div(count, 2))
            def _(q):
                rhs = parts(p)
                for j in range(2):
                    update(first + 4 * q + 2 * j, p, rhs)

            @pl.when(lax.rem(count, 2) == 1)
            def _():
                update(first + 2 * (count - 1), p, parts(p))

        own_loop(s + 1, lambda big: panel_copy(big, s).wait_send())

    for r in range(2):
        others = sum((n - p + 1 - (p + 1 + r) % 2) // 2 for p in range(n))

        @pl.when(jnp.logical_and(my_row == r, aligned))
        def _():
            wait_blocks(others + n * (n + 1) // 2, block_send_sem)

        @pl.when(jnp.logical_and(my_row == r, jnp.logical_not(aligned)))
        def _():
            wait_blocks(2 * others, block_send_sem)

    wait_blocks(n * (n + 1) // 2, out_sem)
    wait_blocks(n * (n - 1) // 2, zero_sem)


def solution(mesh):
    grid_spec = P(("b", "row"), "col")

    def local_factor(a_loc):
        n = a_loc.shape[0]
        W = 2 * NB
        dma = pltpu.SemaphoreType.DMA
        return pl.pallas_call(
            functools.partial(kernel, n),
            out_shape=jax.ShapeDtypeStruct(a_loc.shape, F32),
            in_specs=[pl.BlockSpec(memory_space=pl.ANY)],
            out_specs=pl.BlockSpec(memory_space=pl.ANY),
            scratch_shapes=[
                pltpu.VMEM((n * (n + 1) // 2 * W, W), F32),
                pltpu.VMEM((n * W, W), BF16),
                pltpu.VMEM((n * W, W), BF16),
                pltpu.VMEM((n * W, W), BF16),
                pltpu.VMEM((3, W, W), BF16),
                pltpu.VMEM((NB, NB), F32),
                pltpu.VMEM((NB, NB), F32),
                pltpu.VMEM((2, NB, NB), F32),
                pltpu.VMEM((NB, NB), F32),
                dma((n, n // 2)), dma((n, n // 2)), dma((n, n // 2)), dma((n, n // 2)), dma((n,)), dma((n,)),
                dma, dma((n // 2,)), dma, dma,
            ],
            compiler_params=pltpu.CompilerParams(
                vmem_limit_bytes=60 << 20, collective_id=0, has_side_effects=True),
        )(a_loc)

    return jax.shard_map(local_factor, mesh=mesh, in_specs=grid_spec, out_specs=grid_spec, check_vma=False)
```

time: 721 us -> 327 us (0.45)
  waiting for transfers between devices: 378 us -> 0 us
  Pallas kernels: 329 us -> 315 us
  between operations: 13.4 us -> 0.01 us
  local copies, waits for them, and re-layouts: 0 us -> 11.8 us
    all_gather x2 -> x0, waiting for transfers between devices: 378 us -> none  [local_factor(): gathered = lax.all_gather(lax.all_gather(a_loc, 'col'), 'row')]
    pallas_call x1, Pallas kernels: 329 us -> 315 us  [local_factor(): pl.pallas_call(functools.partial(kernel, n), out_shape=jax.ShapeDtypeStru...]
    unnamed x0 -> x1, local copies, waits for them, and re-layouts: none -> 11.8 us
  transfers between devices with their start and end apart: 2 -> 0, of which waited for: 2 -> 0; matrix products, arithmetic and copies ran while one was open for 0% -> 0% of each run, Pallas kernels for 0% -> 0%
where the time goes in v2:
time: 327 us
  Pallas kernels  315 us (96%)
  local copies, waits for them, and re-layouts  11.8 us (4%)
    pallas_call x1, Pallas kernels, local_factor(): pl.pallas_call(functools.partial(kernel, n), out_shape=jax.ShapeDtypeStru...  315 us
    unnamed x1, local copies, waits for them, and re-layouts  11.8 us

profile of v2, /device:TPU:0, one launch (start us, length us, event | category | flops | bytes accessed | tf_op | source)
XLA Modules:
  0.0 326.7 jit_solution(16904462230092295860)
XLA Ops:
  0.0 314.9 %shard_map.17 = f32[14,14,128,128]{3,2,1,0:T(8,128)} custom-call(f32[14,14,128,128]{3,2,1,0:T(8,128)} %src.1), custom_call_target="tpu_custom_call" | custom-call | tf_op jit(solution)/shard_map/pallas_call | solution.py:378
  314.9 11.8 %copy.3 = f32[14,14,128,128]{3,2,1,0:T(8,128)} copy(f32[14,14,128,128]{3,2,1,0:T(8,128)} %shard_map.17) | data formatting | bytes 25690112

commit v3 on v2

--- a/solution.py
+++ b/solution.py
@@ -82,11 +82,10 @@
             for c in range(SUB):
                 next_main[c] = next_main[c] - below[k] * spread_row(below[k], c)
         if s + 1 < steps:
-            turned = fac.T
             next_ext = spread_cols(rows[s + 1][0], SUB * s)
             for q in range(t + 2, steps):
                 for k in range(SUB):
-                    col = jnp.broadcast_to(turned[SUB * q:SUB * (q + 1), k:k + 1], (SUB, NB))
+                    col = jnp.take_along_axis(fac_rows[k], sub + SUB * q, axis=1)
                     rows[q][0] = rows[q][0] - col * fac_rows[k]
                     rows[q][1] = rows[q][1] - col * inv_rows[k]
                     if q == t + 2:

time: 327 us -> 284 us (0.87)
  Pallas kernels: 315 us -> 272 us
    pallas_call x1, Pallas kernels: 315 us -> 272 us  [local_factor(): pl.pallas_call(functools.partial(kernel, n), out_shape=jax.ShapeDtypeStru...]
where the time goes in v3:
time: 284 us
  Pallas kernels  272 us (96%)
  local copies, waits for them, and re-layouts  11.8 us (4%)
    pallas_call x1, Pallas kernels, local_factor(): pl.pallas_call(functools.partial(kernel, n), out_shape=jax.ShapeDtypeStru...  272 us
    unnamed x1, local copies, waits for them, and re-layouts  11.8 us

profile of v3, /device:TPU:0, one launch (start us, length us, event | category | flops | bytes accessed | tf_op | source)
XLA Modules:
  0.0 283.6 jit_solution(508285097675226188)
XLA Ops:
  0.0 271.8 %shard_map.17 = f32[14,14,128,128]{3,2,1,0:T(8,128)} custom-call(f32[14,14,128,128]{3,2,1,0:T(8,128)} %src.1), custom_call_target="tpu_custom_call" | custom-call | tf_op jit(solution)/shard_map/pallas_call | solution.py:377
  271.8 11.8 %copy.3 = f32[14,14,128,128]{3,2,1,0:T(8,128)} copy(f32[14,14,128,128]{3,2,1,0:T(8,128)} %shard_map.17) | data formatting | bytes 25690112

commit v4 on v3

--- a/solution.py
+++ b/solution.py
@@ -95,13 +95,15 @@
         main = next_main
 
 
-def kernel(n, src, out, tiles, hi, mid, low, invs, upper, blk, blk_inv, zero,
-           loc_sem, sib_sem, nbr_sem, panel_sem, diag_sem, diag_send_sem, block_send_sem, panel_send_sem,
+def kernel(n, src, out, tiles, hi, mid, low, invs, linv, upper, blk, blk_inv, zero,
+           loc_sem, sib_sem, nbr_sem, twin_sem, panel_sem, diag_sem, diag_send_sem, inv_sem, inv_send_sem, block_send_sem, panel_send_sem,
            out_sem, zero_sem):
     W = 2 * NB
     my_row = lax.axis_index("row")
     my_col = lax.axis_index("col")
+    my_rep = lax.axis_index("rep")
     sibling = {"row": 1 - my_row}
+    twin = {"rep": 1 - my_rep}
     aligned = my_row == my_col
     num_own = n // 2
 
@@ -110,7 +112,8 @@
     for core in range(2):
         pl.semaphore_signal(barrier, inc=1, device_id={"col": 1 - my_col, "row": core},
                             device_id_type=pl.DeviceIdType.MESH)
-    pl.semaphore_wait(barrier, 3)
+    pl.semaphore_signal(barrier, inc=1, device_id=twin, device_id_type=pl.DeviceIdType.MESH)
+    pl.semaphore_wait(barrier, 4)
 
     def tile_row(big, p):
         return pl.multiple_of((p * n - (p * (p - 1)) // 2 + big - p) * W, W)
@@ -148,6 +151,9 @@
         @pl.loop(0, count)
         def _(q):
             fn(first + 2 * q)
+
+    def by_x(big, p):
+        return lax.rem(lax.div(big, 2) + p, 2) == my_rep
 
     def local_copy(block, dst, big, p):
         return pltpu.make_async_copy(block, dst, loc_sem.at[p, lax.div(big, 2)])
@@ -182,8 +188,10 @@
         def _():
             @pl.loop(p, n)
             def _(big):
-                remote(src.at[big, p], quadrant(big, p, my_row, my_col), nbr_sem.at[p, lax.div(big, 2)], block_send_sem,
-                       {"col": 1 - my_col, "row": lax.rem(big, 2)}).start()
+                @pl.when(by_x(big, p))
+                def _():
+                    remote(src.at[big, p], quadrant(big, p, my_row, my_col), nbr_sem.at[p, lax.div(big, 2)],
+                           block_send_sem, {"col": 1 - my_col, "row": lax.rem(big, 2)}).start()
 
     @pl.loop(0, n)
     def _(p):
@@ -195,10 +203,31 @@
         ref = tiles.at[pl.ds(0, count * NB // 2), :]
         pltpu.make_async_copy(ref, ref, sem).wait()
 
+    def twin_copy(big, p):
+        half = lax.div(big, 2)
+        block = quadrant(big, p, 1 - my_col, 1 - my_col)
+        return remote(block, block, nbr_sem.at[p, half], twin_sem.at[lax.rem(p, 4), half], twin)
+
+    def forward(p):
+        def one(big):
+            @pl.when(by_x(big, p))
+            def _():
+                wait_blocks(1, nbr_sem.at[p, lax.div(big, 2)])
+                twin_copy(big, p).start()
+
+        own_loop(p, one)
+
     def arrive(p):
         def own(big):
             half = lax.div(big, 2)
-            wait_blocks(1, nbr_sem.at[p, half])
+
+            @pl.when(by_x(big, p))
+            def _():
+                twin_copy(big, p).wait_send()
+
+            @pl.when(jnp.logical_not(by_x(big, p)))
+            def _():
+                wait_blocks(1, nbr_sem.at[p, half])
 
             @pl.when(aligned)
             def _():
@@ -241,6 +270,10 @@
     def diag_copy(s):
         return remote(tile_ref(s, s), tile_ref(s, s), diag_sem.at[s], diag_send_sem.at[s], sibling)
 
+    def inv_copy(s):
+        slot = lax.rem(s, 2)
+        return remote(linv.at[slot], linv.at[slot], inv_sem.at[slot], inv_send_sem, sibling)
+
     def panel_copy(big, s):
         return remote(tile_ref(big, s), tile_ref(big, s), panel_sem.at[s, lax.div(big, 2)], panel_send_sem.at[lax.div(big, 2)], sibling)
 
@@ -249,24 +282,9 @@
         tiles[pl.ds(trow, W), :] = tiles[pl.ds(trow, W), :] - six(dot_nt, parts(big), rhs)
 
     def own(s):
-        return lax.rem(s, 2) == my_row
-
-    arrive(0)
-
-    @pl.when(own(0))
-    def _():
-        diag_copy(0).start()
-
-    @pl.loop(0, n)
-    def _(s):
-        @pl.when(own(s))
-        def _():
-            diag_copy(s).wait_send()
-
-        @pl.when(jnp.logical_not(own(s)))
-        def _():
-            diag_copy(s).wait_recv()
-
+        return lax.rem(s + 2, 2) == my_row
+
+    def factor_tile(s):
         row = tile_row(s, s)
         top, bottom = pl.ds(row, NB), pl.ds(row + NB, NB)
 
@@ -296,14 +314,15 @@
         tiles[top, NB:W] = jnp.zeros((NB, NB), F32)
         l21_parts = split3(tiles[bottom, 0:NB])
         inv1, inv2 = split3(blk_inv[0]), split3(blk_inv[1])
-        cross = six(dot_nn, split3(six(dot_nn, inv2, l21_parts)), inv1)
-        for part in range(3):
-            invs[part, 0:NB, 0:NB] = inv1[part]
-            invs[part, NB:W, NB:W] = inv2[part]
-            invs[part, 0:NB, NB:W] = jnp.zeros((NB, NB), BF16)
-        for part, val in enumerate(split3(-cross)):
-            invs[part, NB:W, 0:NB] = val
-
+        slot = lax.rem(s, 2)
+        linv[slot, NB:W, 0:NB] = -six(dot_nn, split3(six(dot_nn, inv2, l21_parts)), inv1)
+        linv[slot, 0:NB, 0:NB] = blk_inv[0]
+        linv[slot, NB:W, NB:W] = blk_inv[1]
+        linv[slot, 0:NB, NB:W] = jnp.zeros((NB, NB), F32)
+        inv_copy(s).start()
+        diag_copy(s).start()
+
+    def solve_for(s):
         def solve(big):
             trow = tile_row(big, s)
             sol = six(dot_nt, split3(tiles[pl.ds(trow, W), :]), (invs[0], invs[1], invs[2]))
@@ -311,19 +330,15 @@
             panel_copy(big, s).start()
             keep_parts(big, sol)
 
-        own_loop(s + 1, solve)
-
-        @pl.when(jnp.logical_and(s == 0, s + 1 < n))
-        def _():
-            arrive(1)
-
-        @pl.when(jnp.logical_and(own(s + 1), s + 1 < n))
-        def _():
-            update(s + 1, s + 1, parts(s + 1))
-            diag_copy(s + 1).start()
-
+        return solve
+
+    def finish(s):
         other_loop(s + 1, lambda big: panel_copy(big, s).wait_recv())
         other_loop(s + 1, lambda big: keep_parts(big, tiles[pl.ds(tile_row(big, s), W), :]))
+
+        @pl.when(jnp.logical_not(own(s)))
+        def _():
+            diag_copy(s).wait_recv()
 
         @pl.loop(s, n)
         def _(big):
@@ -333,6 +348,10 @@
         def _(p):
             @pl.when(jnp.logical_and(s == 0, p > 1))
             def _():
+                @pl.when(p + 2 < n)
+                def _():
+                    forward(p + 2)
+
                 arrive(p)
 
             first, count = own_tiles(p)
@@ -352,12 +371,58 @@
 
         own_loop(s + 1, lambda big: panel_copy(big, s).wait_send())
 
+    @pl.loop(-1, n)
+    def _(s):
+        @pl.when(s < 0)
+        def _():
+            forward(0)
+            arrive(0)
+
+        @pl.when(s >= 0)
+        def _():
+            @pl.when(jnp.logical_not(own(s)))
+            def _():
+                inv_copy(s).wait_recv()
+
+            for part, val in enumerate(split3(linv[lax.rem(s + 2, 2)])):
+                invs[part] = val
+            own_loop(s + 1, solve_for(s))
+
+        @pl.when(s == 0)
+        def _():
+            arrive(1)
+            forward(3)
+
+        @pl.when(jnp.logical_and(own(s + 1), s + 1 < n))
+        def _():
+            @pl.when(s >= 0)
+            def _():
+                update(s + 1, s + 1, parts(s + 1))
+
+            factor_tile(s + 1)
+
+        @pl.when(s < 0)
+        def _():
+            forward(1)
+            forward(2)
+
+        @pl.when(s >= 0)
+        def _():
+            finish(s)
+
+        @pl.when(jnp.logical_and(own(s + 1), s + 1 < n))
+        def _():
+            inv_copy(s + 1).wait_send()
+            diag_copy(s + 1).wait_send()
+
     for r in range(2):
         others = sum((n - p + 1 - (p + 1 + r) % 2) // 2 for p in range(n))
-
-        @pl.when(jnp.logical_and(my_row == r, aligned))
-        def _():
-            wait_blocks(others + n * (n + 1) // 2, block_send_sem)
+        for copy in range(2):
+            crossing = sum((big // 2 + p) % 2 == copy for p in range(n) for big in range(p, n))
+
+            @pl.when(jnp.logical_and(my_row == r, jnp.logical_and(aligned, my_rep == copy)))
+            def _():
+                wait_blocks(others + crossing, block_send_sem)
 
         @pl.when(jnp.logical_and(my_row == r, jnp.logical_not(aligned)))
         def _():
@@ -385,12 +450,13 @@
                 pltpu.VMEM((n * W, W), BF16),
                 pltpu.VMEM((n * W, W), BF16),
                 pltpu.VMEM((3, W, W), BF16),
+                pltpu.VMEM((2, W, W), F32),
                 pltpu.VMEM((NB, NB), F32),
                 pltpu.VMEM((NB, NB), F32),
                 pltpu.VMEM((2, NB, NB), F32),
                 pltpu.VMEM((NB, NB), F32),
-                dma((n, n // 2)), dma((n, n // 2)), dma((n, n // 2)), dma((n, n // 2)), dma((n,)), dma((n,)),
-                dma, dma((n // 2,)), dma, dma,
+                dma((n, n // 2)), dma((n, n // 2)), dma((n, n // 2)), dma((4, n // 2)), dma((n, n // 2)), dma((n,)), dma((n,)),
+                dma((2,)), dma, dma, dma((n // 2,)), dma, dma,
             ],
             compiler_params=pltpu.CompilerParams(
                 vmem_limit_bytes=60 << 20, collective_id=0, has_side_effects=True),

time: 284 us -> 228 us (0.80)
  Pallas kernels: 272 us -> 216 us
    pallas_call x1, Pallas kernels: 272 us -> 216 us  [local_factor(): pl.pallas_call(functools.partial(kernel, n), out_shape=jax.ShapeDtypeStru...]
where the time goes in v4:
time: 228 us
  Pallas kernels  216 us (95%)
  local copies, waits for them, and re-layouts  11.8 us (5%)
    pallas_call x1, Pallas kernels, local_factor(): pl.pallas_call(functools.partial(kernel, n), out_shape=jax.ShapeDtypeStru...  216 us
    unnamed x1, local copies, waits for them, and re-layouts  11.8 us

profile of v4, /device:TPU:0, one launch (start us, length us, event | category | flops | bytes accessed | tf_op | source)
XLA Modules:
  0.0 227.8 jit_solution(6040973935807691862)
XLA Ops:
  0.0 216.0 %shard_map.17 = f32[14,14,128,128]{3,2,1,0:T(8,128)} custom-call(f32[14,14,128,128]{3,2,1,0:T(8,128)} %src.1), custom_call_target="tpu_custom_call" | custom-call | tf_op jit(solution)/shard_map/pallas_call | solution.py:442
  216.0 11.8 %copy.3 = f32[14,14,128,128]{3,2,1,0:T(8,128)} copy(f32[14,14,128,128]{3,2,1,0:T(8,128)} %shard_map.17) | data formatting | bytes 25690112

commit v5 on v4

--- a/solution.py
+++ b/solution.py
@@ -95,7 +95,7 @@
         main = next_main
 
 
-def kernel(n, src, out, tiles, hi, mid, low, invs, linv, upper, blk, blk_inv, zero,
+def kernel(n, src, out, tiles, hi, mid, low, rhs, invs, linv, upper, blk, blk_inv, zero,
            loc_sem, sib_sem, nbr_sem, twin_sem, panel_sem, diag_sem, diag_send_sem, inv_sem, inv_send_sem, block_send_sem, panel_send_sem,
            out_sem, zero_sem):
     W = 2 * NB
@@ -105,7 +105,6 @@
     sibling = {"row": 1 - my_row}
     twin = {"rep": 1 - my_rep}
     aligned = my_row == my_col
-    num_own = n // 2
 
     barrier = pltpu.get_barrier_semaphore()
     pl.semaphore_signal(barrier, inc=1, device_id=sibling, device_id_type=pl.DeviceIdType.MESH)
@@ -258,12 +257,16 @@
 
         factor_block(lambda t: blk[SUB * t:SUB * (t + 1), :], store)
 
-    def parts(ref_row):
-        row = pl.multiple_of(ref_row * W, W)
+    def kept_row(s, big):
+        half = lax.div(big, 2)
+        return pl.multiple_of((half * half + s) * W, W)
+
+    def parts(s, big):
+        row = kept_row(s, big)
         return tuple(ref[pl.ds(row, W), :] for ref in (hi, mid, low))
 
-    def keep_parts(big, value):
-        row = pl.multiple_of(big * W, W)
+    def keep_parts(s, big, value):
+        row = kept_row(s, big)
         for ref, val in zip((hi, mid, low), split3(value)):
             ref[pl.ds(row, W), :] = val
 
@@ -277,9 +280,9 @@
     def panel_copy(big, s):
         return remote(tile_ref(big, s), tile_ref(big, s), panel_sem.at[s, lax.div(big, 2)], panel_send_sem.at[lax.div(big, 2)], sibling)
 
-    def update(big, p, rhs):
+    def update(s, big, p, right):
         trow = tile_row(big, p)
-        tiles[pl.ds(trow, W), :] = tiles[pl.ds(trow, W), :] - six(dot_nt, parts(big), rhs)
+        tiles[pl.ds(trow, W), :] = tiles[pl.ds(trow, W), :] - six(dot_nt, parts(s, big), right)
 
     def own(s):
         return lax.rem(s + 2, 2) == my_row
@@ -328,13 +331,12 @@
             sol = six(dot_nt, split3(tiles[pl.ds(trow, W), :]), (invs[0], invs[1], invs[2]))
             tiles[pl.ds(trow, W), :] = sol
             panel_copy(big, s).start()
-            keep_parts(big, sol)
+            keep_parts(s, big, sol)
 
         return solve
 
     def finish(s):
         other_loop(s + 1, lambda big: panel_copy(big, s).wait_recv())
-        other_loop(s + 1, lambda big: keep_parts(big, tiles[pl.ds(tile_row(big, s), W), :]))
 
         @pl.when(jnp.logical_not(own(s)))
         def _():
@@ -344,30 +346,37 @@
         def _(big):
             pltpu.make_async_copy(quadrant(big, s, my_row, my_col), out.at[big, s], out_sem).start()
 
-        @pl.loop(s + 1, n)
-        def _(p):
-            @pl.when(jnp.logical_and(s == 0, p > 1))
-            def _():
-                @pl.when(p + 2 < n)
-                def _():
-                    forward(p + 2)
-
-                arrive(p)
-
-            first, count = own_tiles(p)
-            done = jnp.logical_and(p == s + 1, own(p)).astype(jnp.int32)
-            first = first + 2 * done
-            count = count - done
+        def update_column(p, step, first, count):
+            for part, val in enumerate(split3(tiles[pl.ds(tile_row(p, step), W), :])):
+                rhs[part] = val
 
             @pl.loop(0, lax.div(count, 2))
             def _(q):
-                rhs = parts(p)
                 for j in range(2):
-                    update(first + 4 * q + 2 * j, p, rhs)
+                    update(step, first + 4 * q + 2 * j, p, (rhs[0], rhs[1], rhs[2]))
 
             @pl.when(lax.rem(count, 2) == 1)
             def _():
-                update(first + 2 * (count - 1), p, parts(p))
+                update(step, first + 2 * (count - 1), p, (rhs[0], rhs[1], rhs[2]))
+
+        @pl.when(s + 1 < n)
+        def _():
+            first, count = own_tiles(s + 1)
+            done = own(s + 1).astype(jnp.int32)
+            update_column(s + 1, s, first + 2 * done, count - done)
+
+        @pl.when(s + 2 < n)
+        def _():
+            @pl.when(s + 4 < n)
+            def _():
+                forward(s + 4)
+
+            arrive(s + 2)
+            first, count = own_tiles(s + 2)
+
+            @pl.loop(0, s + 1)
+            def _(step):
+                update_column(s + 2, step, first, count)
 
         own_loop(s + 1, lambda big: panel_copy(big, s).wait_send())
 
@@ -397,7 +406,7 @@
         def _():
             @pl.when(s >= 0)
             def _():
-                update(s + 1, s + 1, parts(s + 1))
+                update(s, s + 1, s + 1, parts(s, s + 1))
 
             factor_tile(s + 1)
 
@@ -446,9 +455,10 @@
             out_specs=pl.BlockSpec(memory_space=pl.ANY),
             scratch_shapes=[
                 pltpu.VMEM((n * (n + 1) // 2 * W, W), F32),
-                pltpu.VMEM((n * W, W), BF16),
-                pltpu.VMEM((n * W, W), BF16),
-                pltpu.VMEM((n * W, W), BF16),
+                pltpu.VMEM((n * n // 4 * W, W), BF16),
+                pltpu.VMEM((n * n // 4 * W, W), BF16),
+                pltpu.VMEM((n * n // 4 * W, W), BF16),
+                pltpu.VMEM((3, W, W), BF16),
                 pltpu.VMEM((3, W, W), BF16),
                 pltpu.VMEM((2, W, W), F32),
                 pltpu.VMEM((NB, NB), F32),

time: 228 us -> 216 us (0.947)
  Pallas kernels: 216 us -> 204 us
    pallas_call x1, Pallas kernels: 216 us -> 204 us  [local_factor(): pl.pallas_call(functools.partial(kernel, n), out_shape=jax.ShapeDtypeStru...]
where the time goes in v5:
time: 216 us
  Pallas kernels  204 us (94%)
  local copies, waits for them, and re-layouts  11.8 us (5%)
    pallas_call x1, Pallas kernels, local_factor(): pl.pallas_call(functools.partial(kernel, n), out_shape=jax.ShapeDtypeStru...  204 us
    unnamed x1, local copies, waits for them, and re-layouts  11.8 us

profile of v5, /device:TPU:0, one launch (start us, length us, event | category | flops | bytes accessed | tf_op | source)
XLA Modules:
  0.0 215.8 jit_solution(9768753581959134857)
XLA Ops:
  0.0 204.0 %shard_map.17 = f32[14,14,128,128]{3,2,1,0:T(8,128)} custom-call(f32[14,14,128,128]{3,2,1,0:T(8,128)} %src.1), custom_call_target="tpu_custom_call" | custom-call | tf_op jit(solution)/shard_map/pallas_call | solution.py:451
  204.0 11.8 %copy.3 = f32[14,14,128,128]{3,2,1,0:T(8,128)} copy(f32[14,14,128,128]{3,2,1,0:T(8,128)} %shard_map.17) | data formatting | bytes 25690112

commit v6 on v5

--- a/solution.py
+++ b/solution.py
@@ -336,6 +336,42 @@
         return solve
 
     def finish(s):
+        def update_column(p, step, first, count):
+            def tiles_with(right):
+                @pl.loop(0, lax.div(count, 2))
+                def _(q):
+                    value = right()
+                    for j in range(2):
+                        update(step, first + 4 * q + 2 * j, p, value)
+
+                @pl.when(lax.rem(count, 2) == 1)
+                def _():
+                    update(step, first + 2 * (count - 1), p, right())
+
+            @pl.when(own(p))
+            def _():
+                tiles_with(lambda: parts(step, p))
+
+            @pl.when(jnp.logical_not(own(p)))
+            def _():
+                for part, val in enumerate(split3(tiles[pl.ds(tile_row(p, step), W), :])):
+                    rhs[part] = val
+
+                tiles_with(lambda: (rhs[0], rhs[1], rhs[2]))
+
+        @pl.when(s + 2 < n)
+        def _():
+            @pl.when(s + 4 < n)
+            def _():
+                forward(s + 4)
+
+            arrive(s + 2)
+            first, count = own_tiles(s + 2)
+
+            @pl.loop(0, s)
+            def _(step):
+                update_column(s + 2, step, first, count)
+
         other_loop(s + 1, lambda big: panel_copy(big, s).wait_recv())
 
         @pl.when(jnp.logical_not(own(s)))
@@ -346,19 +382,6 @@
         def _(big):
             pltpu.make_async_copy(quadrant(big, s, my_row, my_col), out.at[big, s], out_sem).start()
 
-        def update_column(p, step, first, count):
-            for part, val in enumerate(split3(tiles[pl.ds(tile_row(p, step), W), :])):
-                rhs[part] = val
-
-            @pl.loop(0, lax.div(count, 2))
-            def _(q):
-                for j in range(2):
-                    update(step, first + 4 * q + 2 * j, p, (rhs[0], rhs[1], rhs[2]))
-
-            @pl.when(lax.rem(count, 2) == 1)
-            def _():
-                update(step, first + 2 * (count - 1), p, (rhs[0], rhs[1], rhs[2]))
-
         @pl.when(s + 1 < n)
         def _():
             first, count = own_tiles(s + 1)
@@ -367,16 +390,8 @@
 
         @pl.when(s + 2 < n)
         def _():
-            @pl.when(s + 4 < n)
-            def _():
-                forward(s + 4)
-
-            arrive(s + 2)
             first, count = own_tiles(s + 2)
-
-            @pl.loop(0, s + 1)
-            def _(step):
-                update_column(s + 2, step, first, count)
+            update_column(s + 2, s, first, count)
 
         own_loop(s + 1, lambda big: panel_copy(big, s).wait_send())
 

time: 216 us -> 214 us (level)
  no operation moved by 1% of the time
where the time goes in v6:
time: 214 us
  Pallas kernels  203 us (95%)
  local copies, waits for them, and re-layouts  11.8 us (6%)
    pallas_call x1, Pallas kernels, local_factor(): pl.pallas_call(functools.partial(kernel, n), out_shape=jax.ShapeDtypeStru...  203 us
    unnamed x1, local copies, waits for them, and re-layouts  11.8 us

profile of v6, /device:TPU:0, one launch (start us, length us, event | category | flops | bytes accessed | tf_op | source)
XLA Modules:
  0.0 214.4 jit_solution(11608082071563065667)
XLA Ops:
  0.0 202.6 %shard_map.17 = f32[14,14,128,128]{3,2,1,0:T(8,128)} custom-call(f32[14,14,128,128]{3,2,1,0:T(8,128)} %src.1), custom_call_target="tpu_custom_call" | custom-call | tf_op jit(solution)/shard_map/pallas_call | solution.py:466
  202.6 11.8 %copy.3 = f32[14,14,128,128]{3,2,1,0:T(8,128)} copy(f32[14,14,128,128]{3,2,1,0:T(8,128)} %shard_map.17) | data formatting | bytes 25690112
